TPU v7x, 32 devices: a whole 2x2x4 slice. The times are simulated.
32 devices in a mesh: dp: 16 (over z, y, core), tensor: 2 (over x).
Axes of the slice: x: 2, y: 2, z: 4, core: 2. Of those that a mesh axis runs over, the one named last changes fastest.
Arguments:
- tokens: bfloat16 [64, 144, 1024], P('dp', 'tensor'), may hold values from -150 to 150
- cotangent: bfloat16 [64, 144, 1024], P('dp', 'tensor'), may hold values from -6 to 6
- dispatch_weight: bfloat16 [1024, 32], replicated, may hold values from -3 to 3
- w_in: bfloat16 [32, 1024, 4096], P('dp', None, 'tensor'), may hold values from -0.1875 to 0.1875
- w_out: bfloat16 [32, 4096, 1024], P('dp', 'tensor'), may hold values from -0.09375 to 0.09375
Outputs:
- grad_tokens: bfloat16 [64, 144, 1024], P('dp', 'tensor')
- grad_router: float32 [1024, 32], replicated
- grad_w_in: bfloat16 [32, 1024, 4096], P('dp', None, 'tensor')
- grad_w_out: bfloat16 [32, 4096, 1024], P('dp', 'tensor')
All inputs are finite; a program needn't handle non-finite values.
Results may differ from a plain program's by a relative error of at most 0.0079.
Values may be sent and summed in bfloat16 or wider, within the bound.
A program may use at most 64 MiB of HBM per device.

v0:
```python
import jax
import jax.numpy as jnp
from jax import lax
from jax.sharding import PartitionSpec as P


def to_experts(partial_rows):
    shared_part = lax.psum_scatter(partial_rows, "tensor", scatter_dimension=2, tiled=True).astype(
        jnp.bfloat16
    )
    arrived = lax.all_to_all(shared_part, "dp", split_axis=1, concat_axis=0, tiled=True)
    result = lax.all_gather(arrived, "tensor", axis=2, tiled=True)
    return result


def to_images(partial_rows):
    shared_part = lax.psum_scatter(partial_rows, "tensor", scatter_dimension=2, tiled=True).astype(
        jnp.bfloat16
    )
    arrived = lax.all_to_all(shared_part, "dp", split_axis=0, concat_axis=1, tiled=True)
    result = lax.all_gather(arrived, "tensor", axis=2, tiled=True)
    return result


def dispatch_softmax(logits):
    local_max = jnp.max(logits, axis=1)
    global_max = lax.pmax(local_max, "tensor")
    exponent = jnp.exp(logits - global_max[:, None, :])
    totals = lax.psum(jnp.sum(exponent, axis=1), "tensor")
    return exponent / totals[:, None, :]


def on_device(tokens, cotangent, dispatch_weight, w_in, w_out):
    wide = jnp.float32
    logits = jnp.einsum("isd,de->ise", tokens, dispatch_weight, preferred_element_type=wide)
    dispatch = dispatch_softmax(logits)
    combine = jax.nn.softmax(logits, axis=2)
    dispatch_low = dispatch.astype(jnp.bfloat16)
    combine_low = combine.astype(jnp.bfloat16)
    slot_inputs = to_experts(
        jnp.einsum("ise,isd->ied", dispatch_low, tokens, preferred_element_type=wide)
    )
    pre_act = jnp.einsum("ied,edf->ief", slot_inputs, w_in, preferred_element_type=wide)
    hidden_act, gelu_back = jax.vjp(jax.nn.gelu, pre_act)
    hidden_low = hidden_act.astype(jnp.bfloat16)
    slot_outputs = to_images(
        jnp.einsum("ief,efd->ied", hidden_low, w_out, preferred_element_type=wide)
    )
    grad_combine = jnp.einsum("isd,ied->ise", cotangent, slot_outputs, preferred_element_type=wide)
    grad_slots_out = to_experts(
        jnp.einsum("ise,isd->ied", combine_low, cotangent, preferred_element_type=wide)
    )
    grad_hidden = jnp.einsum("ied,efd->ief", grad_slots_out, w_out, preferred_element_type=wide)
    grad_pre = gelu_back(grad_hidden)[0].astype(jnp.bfloat16)
    grad_w_out = jnp.einsum(
        "ief,ied->efd", hidden_low, grad_slots_out, preferred_element_type=wide
    ).astype(jnp.bfloat16)
    grad_w_in = jnp.einsum(
        "ied,ief->edf", slot_inputs, grad_pre, preferred_element_type=wide
    ).astype(jnp.bfloat16)
    grad_slots_in = to_images(
        jnp.einsum("ief,edf->ied", grad_pre, w_in, preferred_element_type=wide)
    )
    grad_dispatch = jnp.einsum("isd,ied->ise", tokens, grad_slots_in, preferred_element_type=wide)
    column_dot = lax.psum(jnp.sum(grad_dispatch * dispatch, axis=1), "tensor")
    row_dot = jnp.sum(grad_combine * combine, axis=2, keepdims=True)
    grad_logits = (
        combine * (grad_combine - row_dot) + dispatch * (grad_dispatch - column_dot[:, None, :])
    ).astype(jnp.bfloat16)
    token_part = jnp.einsum(
        "ise,ied->isd", dispatch_low, grad_slots_in, preferred_element_type=wide
    )
    router_part = jnp.einsum(
        "ise,de->isd", grad_logits, dispatch_weight, preferred_element_type=wide
    )
    grad_tokens = (token_part + router_part).astype(jnp.bfloat16)
    local_router = jnp.einsum("isd,ise->de", tokens, grad_logits, preferred_element_type=wide)
    grad_router = lax.psum(local_router, ("dp", "tensor"))
    return (grad_tokens, grad_router, grad_w_in, grad_w_out)


def solution(mesh):
    return jax.shard_map(
        on_device,
        mesh=mesh,
        in_specs=(
            P("dp", "tensor", None),
            P("dp", "tensor", None),
            P(),
            P("dp", None, "tensor"),
            P("dp", "tensor", None),
        ),
        out_specs=(P("dp", "tensor", None), P(), P("dp", None, "tensor"), P("dp", "tensor", None)),
        check_vma=False,
    )
```

profile of v0, /device:TPU:0, one launch (start us, length us, event | category | flops | bytes accessed | tf_op | source)
XLA Modules:
  0.0 270.4 jit_solution(4491643558524088509)
XLA Ops:
  7.2 0.0 copy-start
  7.2 0.0 reduce-scatter.5.cloned.1.call-start
  7.2 1.0 copy-done
  8.2 1.3 fusion.37
  9.5 0.2 fusion.38
  9.7 2.1 fusion.26
  11.8 0.0 reduce-scatter.5.cloned.1.call-update
  11.8 0.0 reduce-scatter.7.cloned.1.call-start
  11.9 5.9 %pmax.7 = f32[4,32]{1,0:T(4,128)S(1)} all-reduce(f32[4,32]{1,0:T(4,128)S(1)} %get-tuple-element.4), channel_id=1, replica_groups=mesh['dp'=16,'tensor'=2] {'tensor'}, use_global_device_ids=true, to_apply=%region_1.0 | all-reduce | flops 128 | bytes 1024 | tf_op jit(solution)/shard_map/pmax | solution.py:27
  17.7 0.2 fusion.25
  17.9 4.9 %psum.21 = f32[4,32]{1,0:T(4,128)S(1)} all-reduce(f32[4,32]{1,0:T(4,128)S(1)} %fusion.25), channel_id=1, replica_groups=mesh['dp'=16,'tensor'=2] {'tensor'}, use_global_device_ids=true, to_apply=%region_3.0 | all-reduce | flops 128 | bytes 1024 | tf_op jit(solution)/shard_map/psum | solution.py:29
  22.9 1.1 fusion.29
  24.0 0.0 reduce-scatter.7.cloned.1.call-update
  24.0 5.4 %reduce-scatter.5.cloned.1.call-done = f32[4,32,512]{2,1,0:T(8,128)} async-done(((f32[4,32,1024]{2,1,0:T(8,128)}), f32[4,32,512]{2,1,0:T(8,128)}) %reduce-scatter.5.cloned.1.call-update) | async-done | bytes 262160 | tf_op jit(solution)/shard_map/reduce_scatter | solution.py:8
  29.4 1.0 convert_element_type.38
  30.3 0.8 copy.13
  31.1 5.6 %all-to-all-start = ((bf16[4,32,512]{2,0,1:T(4,128)(2,1)}), bf16[4,32,512]{2,0,1:T(4,128)(2,1)S(1)}, u32[]{:S(2)}, u32[]{:S(2)}) async-start(bf16[4,32,512]{2,0,1:T(4,128)(2,1)} %copy.13), calls=%async_computation.1 | async-start | bytes 262144 | tf_op jit(solution)/shard_map/all_to_all | solution.py:11
  36.7 10.1 %reduce-scatter.7.cloned.1.call-done = f32[4,32,512]{2,1,0:T(8,128)} async-done(((f32[4,32,1024]{2,1,0:T(8,128)}), f32[4,32,512]{2,1,0:T(8,128)}) %reduce-scatter.7.cloned.1.call-update) | async-done | bytes 262160 | tf_op jit(solution)/shard_map/reduce_scatter | solution.py:8
  46.9 1.0 convert_element_type.39
  47.8 0.8 copy.15
  48.6 0.0 all-to-all-done
  48.6 5.6 %all-to-all-start.1 = ((bf16[4,32,512]{2,0,1:T(4,128)(2,1)}), bf16[4,32,512]{2,0,1:T(4,128)(2,1)S(1)}, u32[]{:S(2)}, u32[]{:S(2)}) async-start(bf16[4,32,512]{2,0,1:T(4,128)(2,1)} %copy.15), calls=%async_computation.3 | async-start | bytes 262144 | tf_op jit(solution)/shard_map/all_to_all | solution.py:11
  54.2 0.0 reduce-scatter.9.cloned.1.call-start
  54.4 6.5 %all_gather.12 = bf16[64,2,1024]{2,0,1:T(8,128)(2,1)S(1)} all-gather(bf16[64,2,512]{2,0,1:T(8,128)(2,1)S(1)} %all_to_all.55), channel_id=1, replica_groups=mesh['dp'=16,'tensor'=2] {'tensor'}, dimensions={2}, use_global_device_ids=true | all-gather | bytes 393216 | tf_op jit(solution)/shard_map/all_gather | solution.py:12
  60.8 1.3 all-to-all-done.1
  62.2 0.0 copy-start.1
  62.2 0.0 slice-start
  62.2 5.8 %all_gather.13 = bf16[64,2,1024]{2,0,1:T(8,128)(2,1)S(1)} all-gather(bf16[64,2,512]{2,0,1:T(8,128)(2,1)S(1)} %all_to_all.59), channel_id=1, replica_groups=mesh['dp'=16,'tensor'=2] {'tensor'}, dimensions={2}, use_global_device_ids=true | all-gather | bytes 393216 | tf_op jit(solution)/shard_map/all_gather | solution.py:12
  68.0 5.1 %convolution_bitcast_fusion = f32[64,2,2048]{2,0,1:T(8,128)S(1)} fusion(bf16[64,2,1024]{2,0,1:T(8,128)(2,1)S(1)} %all_gather.13, bf16[2,1024,2048]{2,1,0:T(8,128)(2,1)} %param.8), kind=kOutput, calls=%fused_computation.4 | convolution fusion | flops 536870912 | bytes 9699328 | tf_op jit(solution)/shard_map/ied,edf->ief/dot_general | solution.py:43
  73.1 2.9 %fusion.16 = bf16[64,2,2048]{2,0,1:T(8,128)(2,1)S(1)} fusion(f32[64,2,2048]{2,0,1:T(8,128)S(1)} %convolution_bitcast_fusion, bf16[64,2,1024]{2,0,1:T(8,128)(2,1)S(1)} %all_gather.12, bf16[2,2048,1024]{2,1,0:T(8,128)(2,1)S(1)} %copy-done.1), kind=kOutput, calls=%fused_computation.28 | convolution fusion | flops 542113792 | bytes 10223616 | tf_op jit(solution)/shard_map/ied,efd->ief/dot_general | solution.py:53
  76.0 3.5 %convolution_bitcast_fusion.3 = f32[64,2,1024]{2,0,1:T(8,128)} fusion(bf16[64,2,2048]{2,0,1:T(8,128)(2,1)S(1)} %fusion.16, bf16[2,1024,2048]{2,1,0:T(8,128)(2,1)S(1)} %bitcast.67), kind=kOutput, calls=%fused_computation.11 | convolution fusion | flops 536870912 | bytes 9437184 | tf_op jit(solution)/shard_map/ief,edf->ied/dot_general | solution.py:62
  79.5 0.0 reduce-scatter.9.cloned.1.call-update
  79.5 0.0 reduce-scatter.11.cloned.1.call-start
  79.6 5.7 %convolution_bitcast_fusion.2 = f32[64,2,1024]{2,0,1:T(8,128)} fusion(bf16[2,2048,1024]{2,1,0:T(8,128)(2,1)} %param.9, f32[64,2,2048]{2,0,1:T(8,128)S(1)} %convolution_bitcast_fusion), kind=kOutput, calls=%fused_computation.10 | convolution fusion | flops 539230208 | bytes 9961472 | tf_op jit(solution)/shard_map/ief,efd->ied/dot_general | solution.py:47
  85.3 0.0 reduce-scatter.11.cloned.1.call-update
  85.3 5.8 %convolution_convert_fusion = bf16[2,2048,1024]{2,1,0:T(8,128)(2,1)} fusion(bf16[64,2,1024]{2,0,1:T(8,128)(2,1)S(1)} %all_gather.12, f32[64,2,2048]{2,0,1:T(8,128)S(1)} %convolution_bitcast_fusion), kind=kOutput, calls=%fused_computation.2 | convolution fusion | flops 543424512 | bytes 9699328 | tf_op jit(solution)/shard_map/ief,ied->efd/dot_general | solution.py:55
  91.1 2.0 reduce-scatter.9.cloned.1.call-done
  93.1 1.0 convert_element_type.41
  94.1 0.8 copy.17
  94.9 5.6 %all-to-all-start.2 = ((bf16[64,2,512]{2,1,0:T(2,128)(2,1)}), bf16[64,2,512]{2,1,0:T(2,128)(2,1)S(1)}, u32[]{:S(2)}, u32[]{:S(2)}) async-start(bf16[64,2,512]{2,1,0:T(2,128)(2,1)} %copy.17), calls=%async_computation.5 | async-start | bytes 262144 | tf_op jit(solution)/shard_map/all_to_all | solution.py:20
  100.5 5.8 %convolution_convert_fusion.1 = bf16[2,1024,2048]{2,1,0:T(8,128)(2,1)} fusion(bf16[64,2,1024]{2,0,1:T(8,128)(2,1)S(1)} %all_gather.13, bf16[64,2,2048]{2,0,1:T(8,128)(2,1)S(1)} %fusion.16), kind=kOutput, calls=%fused_computation.3 | convolution fusion | flops 541065216 | bytes 9175040 | tf_op jit(solution)/shard_map/ied,ief->edf/dot_general | solution.py:58
  106.3 4.2 %reduce-scatter.11.cloned.1.call-done = f32[64,2,512]{2,0,1:T(8,128)} async-done(((f32[64,2,1024]{2,0,1:T(8,128)}), f32[64,2,512]{2,0,1:T(8,128)}) %reduce-scatter.11.cloned.1.call-update) | async-done | bytes 262160 | tf_op jit(solution)/shard_map/reduce_scatter | solution.py:17
  110.4 1.0 convert_element_type.43
  111.4 0.8 copy.19
  112.2 0.0 all-to-all-done.2
  112.2 5.6 %all-to-all-start.3 = ((bf16[64,2,512]{2,1,0:T(2,128)(2,1)}), bf16[64,2,512]{2,1,0:T(2,128)(2,1)S(1)}, u32[]{:S(2)}, u32[]{:S(2)}) async-start(bf16[64,2,512]{2,1,0:T(2,128)(2,1)} %copy.19), calls=%async_computation.7 | async-start | bytes 262144 | tf_op jit(solution)/shard_map/all_to_all | solution.py:20
  117.9 0.0 all-reduce.2.cloned.1.call-start
  117.9 0.1 copy.26
  118.0 0.1 all_to_all.63
  118.1 6.5 %all_gather.14 = bf16[4,32,1024]{2,1,0:T(8,128)(2,1)S(1)} all-gather(bf16[4,32,512]{2,1,0:T(8,128)(2,1)S(1)} %all_to_all.63), channel_id=1, replica_groups=mesh['dp'=16,'tensor'=2] {'tensor'}, dimensions={2}, use_global_device_ids=true | all-gather | bytes 393216 | tf_op jit(solution)/shard_map/all_gather | solution.py:21
  124.5 0.4 multiply_reduce_fusion.1
  124.9 4.9 %psum.22 = f32[4,32]{1,0:T(4,128)S(1)} all-reduce(f32[4,32]{1,0:T(4,128)S(1)} %get-tuple-element.8), channel_id=1, replica_groups=mesh['dp'=16,'tensor'=2] {'tensor'}, use_global_device_ids=true, to_apply=%region_12.0 | all-reduce | flops 128 | bytes 1024 | tf_op jit(solution)/shard_map/psum | solution.py:65
  129.8 0.0 all-to-all-done.3
  129.9 0.1 copy.25
  129.9 0.1 all_to_all.67
  130.0 5.6 %all_gather.15 = bf16[4,32,1024]{2,1,0:T(8,128)(2,1)S(1)} all-gather(bf16[4,32,512]{2,1,0:T(8,128)(2,1)S(1)} %all_to_all.67), channel_id=1, replica_groups=mesh['dp'=16,'tensor'=2] {'tensor'}, dimensions={2}, use_global_device_ids=true | all-gather | bytes 393216 | tf_op jit(solution)/shard_map/all_gather | solution.py:21
  135.6 0.0 copy-done.2
  135.7 0.3 convolution_bitcast_fusion.6
  135.9 1.0 convolution_bitcast_fusion.4
  137.0 0.4 fusion.9
  137.4 0.0 all-reduce.2.cloned.1.call-update
  137.5 1.3 fusion.2
  138.7 123.5 %all-reduce.2.cloned.1.call-done = f32[1024,32]{0,1:T(8,128)} async-done(((f32[1024,32]{0,1:T(8,128)}), f32[1024,32]{0,1:T(8,128)}) %all-reduce.2.cloned.1.call-update) | async-done | bytes 131088 | tf_op jit(solution)/shard_map/psum | solution.py:78
  262.3 1.6 copy.30
  (12 shorter events, 0.2 us)
Async XLA Ops:
  7.2 1.1 copy-start
  7.2 22.2 %reduce-scatter.5.cloned.1.call-start = ((), (), s32[]{:S(2)}) async-start(), calls=%async_computation.8 | async-start | bytes 786432 | tf_op jit(solution)/shard_map/reduce_scatter | solution.py:8
  11.8 35.0 %reduce-scatter.7.cloned.1.call-start = ((), (), s32[]{:S(2)}) async-start(), calls=%async_computation.9 | async-start | bytes 786432 | tf_op jit(solution)/shard_map/reduce_scatter | solution.py:8
  31.1 17.5 %all-to-all-start = ((bf16[4,32,512]{2,0,1:T(4,128)(2,1)}), bf16[4,32,512]{2,0,1:T(4,128)(2,1)S(1)}, u32[]{:S(2)}, u32[]{:S(2)}) async-start(bf16[4,32,512]{2,0,1:T(4,128)(2,1)} %copy.13), calls=%async_computation.1 | async-start | bytes 262144 | tf_op jit(solution)/shard_map/all_to_all | solution.py:11
  48.6 13.5 %all-to-all-start.1 = ((bf16[4,32,512]{2,0,1:T(4,128)(2,1)}), bf16[4,32,512]{2,0,1:T(4,128)(2,1)S(1)}, u32[]{:S(2)}, u32[]{:S(2)}) async-start(bf16[4,32,512]{2,0,1:T(4,128)(2,1)} %copy.15), calls=%async_computation.3 | async-start | bytes 262144 | tf_op jit(solution)/shard_map/all_to_all | solution.py:11
  54.2 38.9 %reduce-scatter.9.cloned.1.call-start = ((), (), s32[]{:S(2)}) async-start(), calls=%async_computation.10 | async-start | bytes 786432 | tf_op jit(solution)/shard_map/reduce_scatter | solution.py:17
  62.2 10.9 %copy-start.1 = (bf16[2,2048,1024]{2,1,0:T(8,128)(2,1)S(1)}, bf16[2,2048,1024]{2,1,0:T(8,128)(2,1)}, u32[]{:S(2)}) copy-start(bf16[2,2048,1024]{2,1,0:T(8,128)(2,1)} %param.9) | copy-start | bytes 25165828
  62.2 13.8 %slice-start = ((s8[8388608]{0:T(1024)(128)(4,1)}), s8[4194304]{0:T(1024)(128)(4,1)S(1)}, s32[]{:S(2)}) async-start(s8[8388608]{0:T(1024)(128)(4,1)} %bitcast.66), calls=%async_computation.13 | async-start | bytes 8388608
  68.0 8.0 %slice-start.1 = ((s8[8388608]{0:T(1024)(128)(4,1)}), s8[4194304]{0:T(1024)(128)(4,1)S(1)}, s32[]{:S(2)}) async-start(s8[8388608]{0:T(1024)(128)(4,1)} %bitcast.66), calls=%async_computation.14 | async-start | bytes 8388608
  79.5 30.9 %reduce-scatter.11.cloned.1.call-start = ((), (), s32[]{:S(2)}) async-start(), calls=%async_computation.11 | async-start | bytes 786432 | tf_op jit(solution)/shard_map/reduce_scatter | solution.py:17
  91.1 44.6 %copy-start.2 = (bf16[4,72,1024]{2,1,0:T(8,128)(2,1)S(1)}, bf16[4,72,1024]{2,1,0:T(8,128)(2,1)}, u32[]{:S(2)}) copy-start(bf16[4,72,1024]{2,1,0:T(8,128)(2,1)} %param.6) | copy-start | bytes 1769476
  91.1 45.9 %copy-start.3 = (bf16[1024,32]{0,1:T(8,128)(2,1)S(1)}, bf16[1024,32]{0,1:T(8,128)(2,1)}, u32[]{:S(2)}) copy-start(bf16[1024,32]{0,1:T(8,128)(2,1)} %param.7) | copy-start | bytes 196612
  94.9 17.3 %all-to-all-start.2 = ((bf16[64,2,512]{2,1,0:T(2,128)(2,1)}), bf16[64,2,512]{2,1,0:T(2,128)(2,1)S(1)}, u32[]{:S(2)}, u32[]{:S(2)}) async-start(bf16[64,2,512]{2,1,0:T(2,128)(2,1)} %copy.17), calls=%async_computation.5 | async-start | bytes 262144 | tf_op jit(solution)/shard_map/all_to_all | solution.py:20
  112.2 17.6 %all-to-all-start.3 = ((bf16[64,2,512]{2,1,0:T(2,128)(2,1)}), bf16[64,2,512]{2,1,0:T(2,128)(2,1)S(1)}, u32[]{:S(2)}, u32[]{:S(2)}) async-start(bf16[64,2,512]{2,1,0:T(2,128)(2,1)} %copy.19), calls=%async_computation.7 | async-start | bytes 262144 | tf_op jit(solution)/shard_map/all_to_all | solution.py:20
  117.9 144.4 %all-reduce.2.cloned.1.call-start = ((), (), s32[]{:S(2)}) async-start(), calls=%async_computation.12 | async-start | bytes 262144 | tf_op jit(solution)/shard_map/psum | solution.py:78
Sparse Core Ops, SparseCore 0:
  11.9 17.3 reduce-scatter.4
  32.2 14.6 reduce-scatter.6
  79.6 13.4 reduce-scatter.8
  95.8 14.6 reduce-scatter.10
  137.6 124.6 all-reduce.1
where the time goes:
time: 271 us; the launch traced here: 270 us
  waiting for transfers between devices  147 us (54%)
  blocking collectives  40.1 us (15%)
  matrix products  36.6 us (14%)
  starting transfers between devices  22.7 us (8%)
  between operations  14 us (5%)
  local copies, waits for them, and re-layouts  6.18 us (2%)
  other arithmetic  4.2 us (2%)
    psum x1, waiting for transfers between devices, on_device(): grad_router = lax.psum(local_router, ('dp', 'tensor'))  124 us
    reduce_scatter x2, waiting for transfers between devices, to_experts(): lax.psum_scatter(partial_rows, 'tensor', scatter_dimension=2, tiled=True)  15.5 us
    all_gather x2, blocking collectives, to_experts(): result = lax.all_gather(arrived, 'tensor', axis=2, tiled=True)  12.2 us
    all_gather x2, blocking collectives, to_images(): result = lax.all_gather(arrived, 'tensor', axis=2, tiled=True)  12.1 us
    all_to_all x2, starting transfers between devices, to_images(): lax.all_to_all(shared_part, 'dp', split_axis=0, concat_axis=1, tiled=True)  11.3 us
    all_to_all x2, starting transfers between devices, to_experts(): lax.all_to_all(shared_part, 'dp', split_axis=1, concat_axis=0, tiled=True)  11.2 us
    reduce_scatter x2, waiting for transfers between devices, to_images(): lax.psum_scatter(partial_rows, 'tensor', scatter_dimension=2, tiled=True)  6.15 us
    pmax x1, blocking collectives, dispatch_softmax(): global_max = lax.pmax(local_max, 'tensor')  5.87 us
  transfers between devices with their start and end apart: 9, of which 6 were waited for; matrix products, arithmetic and copies ran while one was open for 10% of the time, Pallas kernels for 0%

commit v1 on v0

--- a/solution.py
+++ b/solution.py
@@ -75,7 +75,7 @@
     )
     grad_tokens = (token_part + router_part).astype(jnp.bfloat16)
     local_router = jnp.einsum("isd,ise->de", tokens, grad_logits, preferred_element_type=wide)
-    grad_router = lax.psum(local_router, ("dp", "tensor"))
+    grad_router = jnp.sum(lax.all_gather(local_router, ("dp", "tensor")), 0)
     return (grad_tokens, grad_router, grad_w_in, grad_w_out)
 
 

time: 271 us -> 217 us (0.80)
  waiting for transfers between devices: 147 us -> 82.9 us
  local copies, waits for them, and re-layouts: 6.18 us -> 11.7 us
    psum x1 -> x0, waiting for transfers between devices: 124 us -> none  [on_device(): grad_router = lax.psum(local_router, ('dp', 'tensor'))]
    all_gather x0 -> x1, waiting for transfers between devices: none -> 48.4 us  [on_device(): grad_router = jnp.sum(lax.all_gather(local_router, ('dp', 'tensor')), 0)]
    reduce_scatter x2, waiting for transfers between devices: 6.15 us -> 17.7 us  [to_images(): lax.psum_scatter(partial_rows, 'tensor', scatter_dimension=2, tiled=True)]
    unnamed x13 -> x17, local copies, waits for them, and re-layouts: 2.61 us -> 5.67 us
  transfers between devices with their start and end apart: 9 -> 9, of which waited for: 6 -> 6; matrix products, arithmetic and copies ran while one was open for 10% -> 13% of each run, Pallas kernels for 0% -> 0%
where the time goes in v1:
time: 217 us; the launch traced here: 216 us
  waiting for transfers between devices  82.9 us (38%)
  blocking collectives  40.2 us (19%)
  matrix products  38.5 us (18%)
  starting transfers between devices  22.8 us (11%)
  between operations  14 us (6%)
  local copies, waits for them, and re-layouts  11.7 us (5%)
  other arithmetic  5.95 us (3%)
    all_gather x1, waiting for transfers between devices, on_device(): grad_router = jnp.sum(lax.all_gather(local_router, ('dp', 'tensor')), 0)  48.4 us
    reduce_scatter x2, waiting for transfers between devices, to_images(): lax.psum_scatter(partial_rows, 'tensor', scatter_dimension=2, tiled=True)  17.7 us
    reduce_scatter x2, waiting for transfers between devices, to_experts(): lax.psum_scatter(partial_rows, 'tensor', scatter_dimension=2, tiled=True)  15.5 us
    all_gather x2, blocking collectives, to_experts(): result = lax.all_gather(arrived, 'tensor', axis=2, tiled=True)  12.2 us
    all_gather x2, blocking collectives, to_images(): result = lax.all_gather(arrived, 'tensor', axis=2, tiled=True)  12.2 us
    all_to_all x2, starting transfers between devices, to_images(): lax.all_to_all(shared_part, 'dp', split_axis=0, concat_axis=1, tiled=True)  11.3 us
    all_to_all x2, starting transfers between devices, to_experts(): lax.all_to_all(shared_part, 'dp', split_axis=1, concat_axis=0, tiled=True)  11.2 us
    pmax x1, blocking collectives, dispatch_softmax(): global_max = lax.pmax(local_max, 'tensor')  5.87 us
  transfers between devices with their start and end apart: 9, of which 6 were waited for; matrix products, arithmetic and copies ran while one was open for 13% of the time, Pallas kernels for 0%

profile of v1, /device:TPU:0, one launch (start us, length us, event | category | flops | bytes accessed | tf_op | source)
XLA Modules:
  0.0 216.1 jit_solution(2641665952350378834)
XLA Ops:
  7.2 0.0 copy-start
  7.2 0.0 reduce-scatter.5.cloned.1.call-start
  7.2 1.0 copy-done
  8.2 1.3 fusion.37
  9.5 0.6 fusion.38
  10.2 2.1 fusion.26
  12.3 0.0 reduce-scatter.5.cloned.1.call-update
  12.3 0.0 reduce-scatter.7.cloned.1.call-start
  12.4 5.9 %pmax.7 = f32[4,32]{1,0:T(4,128)S(1)} all-reduce(f32[4,32]{1,0:T(4,128)S(1)} %get-tuple-element.4), channel_id=1, replica_groups=mesh['dp'=16,'tensor'=2] {'tensor'}, use_global_device_ids=true, to_apply=%region_1.0 | all-reduce | flops 128 | bytes 1024 | tf_op jit(solution)/shard_map/pmax | solution.py:27
  18.2 0.2 fusion.25
  18.4 4.9 %psum.14 = f32[4,32]{1,0:T(4,128)S(1)} all-reduce(f32[4,32]{1,0:T(4,128)S(1)} %fusion.25), channel_id=1, replica_groups=mesh['dp'=16,'tensor'=2] {'tensor'}, use_global_device_ids=true, to_apply=%region_3.0 | all-reduce | flops 128 | bytes 1024 | tf_op jit(solution)/shard_map/psum | solution.py:29
  23.3 1.1 fusion.29
  24.4 0.0 reduce-scatter.7.cloned.1.call-update
  24.5 5.4 %reduce-scatter.5.cloned.1.call-done = f32[4,32,512]{2,1,0:T(8,128)} async-done(((f32[4,32,1024]{2,1,0:T(8,128)}), f32[4,32,512]{2,1,0:T(8,128)}) %reduce-scatter.5.cloned.1.call-update) | async-done | bytes 262160 | tf_op jit(solution)/shard_map/reduce_scatter | solution.py:8
  29.8 1.0 convert_element_type.38
  30.8 0.8 copy.13
  31.6 5.6 %all-to-all-start = ((bf16[4,32,512]{2,0,1:T(4,128)(2,1)}), bf16[4,32,512]{2,0,1:T(4,128)(2,1)S(1)}, u32[]{:S(2)}, u32[]{:S(2)}) async-start(bf16[4,32,512]{2,0,1:T(4,128)(2,1)} %copy.13), calls=%async_computation.1 | async-start | bytes 262144 | tf_op jit(solution)/shard_map/all_to_all | solution.py:11
  37.2 10.1 %reduce-scatter.7.cloned.1.call-done = f32[4,32,512]{2,1,0:T(8,128)} async-done(((f32[4,32,1024]{2,1,0:T(8,128)}), f32[4,32,512]{2,1,0:T(8,128)}) %reduce-scatter.7.cloned.1.call-update) | async-done | bytes 262160 | tf_op jit(solution)/shard_map/reduce_scatter | solution.py:8
  47.3 1.0 convert_element_type.39
  48.3 0.8 copy.15
  49.1 5.6 %all-to-all-start.1 = ((bf16[4,32,512]{2,0,1:T(4,128)(2,1)}), bf16[4,32,512]{2,0,1:T(4,128)(2,1)S(1)}, u32[]{:S(2)}, u32[]{:S(2)}) async-start(bf16[4,32,512]{2,0,1:T(4,128)(2,1)} %copy.15), calls=%async_computation.3 | async-start | bytes 262144 | tf_op jit(solution)/shard_map/all_to_all | solution.py:11
  54.7 0.0 reduce-scatter.9.cloned.1.call-start
  54.8 6.5 %all_gather.18 = bf16[64,2,1024]{2,0,1:T(8,128)(2,1)S(1)} all-gather(bf16[64,2,512]{2,0,1:T(8,128)(2,1)S(1)} %all_to_all.55), channel_id=1, replica_groups=mesh['dp'=16,'tensor'=2] {'tensor'}, dimensions={2}, use_global_device_ids=true | all-gather | bytes 393216 | tf_op jit(solution)/shard_map/all_gather | solution.py:12
  61.3 1.3 all-to-all-done.1
  62.7 0.0 copy-start.1
  62.7 0.0 slice-start
  62.7 5.8 %all_gather.19 = bf16[64,2,1024]{2,0,1:T(8,128)(2,1)S(1)} all-gather(bf16[64,2,512]{2,0,1:T(8,128)(2,1)S(1)} %all_to_all.59), channel_id=1, replica_groups=mesh['dp'=16,'tensor'=2] {'tensor'}, dimensions={2}, use_global_device_ids=true | all-gather | bytes 393216 | tf_op jit(solution)/shard_map/all_gather | solution.py:12
  68.5 5.1 %convolution_bitcast_fusion = f32[64,2,2048]{2,0,1:T(8,128)S(1)} fusion(bf16[64,2,1024]{2,0,1:T(8,128)(2,1)S(1)} %all_gather.19, bf16[2,1024,2048]{2,1,0:T(8,128)(2,1)} %param.8), kind=kOutput, calls=%fused_computation.5 | convolution fusion | flops 536870912 | bytes 9699328 | tf_op jit(solution)/shard_map/ied,edf->ief/dot_general | solution.py:43
  73.6 2.9 %fusion.16 = bf16[64,2,2048]{2,0,1:T(8,128)(2,1)S(1)} fusion(f32[64,2,2048]{2,0,1:T(8,128)S(1)} %convolution_bitcast_fusion, bf16[64,2,1024]{2,0,1:T(8,128)(2,1)S(1)} %all_gather.18, bf16[2,2048,1024]{2,1,0:T(8,128)(2,1)S(1)} %copy-done.1), kind=kOutput, calls=%fused_computation.29 | convolution fusion | flops 542113792 | bytes 10223616 | tf_op jit(solution)/shard_map/ied,efd->ief/dot_general | solution.py:53
  76.5 3.5 %convolution_bitcast_fusion.3 = f32[64,2,1024]{2,0,1:T(8,128)} fusion(bf16[64,2,2048]{2,0,1:T(8,128)(2,1)S(1)} %fusion.16, bf16[2,1024,2048]{2,1,0:T(8,128)(2,1)S(1)} %bitcast.72), kind=kOutput, calls=%fused_computation.12 | convolution fusion | flops 536870912 | bytes 9437184 | tf_op jit(solution)/shard_map/ief,edf->ied/dot_general | solution.py:62
  80.0 0.0 reduce-scatter.9.cloned.1.call-update
  80.0 0.0 copy-start.2
  80.0 0.0 reduce-scatter.11.cloned.1.call-start
  80.1 5.8 %convolution_bitcast_fusion.2 = f32[64,2,1024]{2,0,1:T(8,128)} fusion(bf16[2,2048,1024]{2,1,0:T(8,128)(2,1)} %param.9, f32[64,2,2048]{2,0,1:T(8,128)S(1)} %convolution_bitcast_fusion), kind=kOutput, calls=%fused_computation.11 | convolution fusion | flops 539230208 | bytes 9961472 | tf_op jit(solution)/shard_map/ief,efd->ied/dot_general | solution.py:47
  85.8 0.0 reduce-scatter.11.cloned.1.call-update
  85.9 7.7 %reduce-scatter.9.cloned.1.call-done = f32[64,2,512]{2,0,1:T(8,128)} async-done(((f32[64,2,1024]{2,0,1:T(8,128)}), f32[64,2,512]{2,0,1:T(8,128)}) %reduce-scatter.9.cloned.1.call-update) | async-done | bytes 262160 | tf_op jit(solution)/shard_map/reduce_scatter | solution.py:17
  93.6 1.0 convert_element_type.41
  94.6 0.8 copy.17
  95.3 5.6 %all-to-all-start.2 = ((bf16[64,2,512]{2,1,0:T(2,128)(2,1)}), bf16[64,2,512]{2,1,0:T(2,128)(2,1)S(1)}, u32[]{:S(2)}, u32[]{:S(2)}) async-start(bf16[64,2,512]{2,1,0:T(2,128)(2,1)} %copy.17), calls=%async_computation.5 | async-start | bytes 262144 | tf_op jit(solution)/shard_map/all_to_all | solution.py:20
  101.0 9.9 %reduce-scatter.11.cloned.1.call-done = f32[64,2,512]{2,0,1:T(8,128)} async-done(((f32[64,2,1024]{2,0,1:T(8,128)}), f32[64,2,512]{2,0,1:T(8,128)}) %reduce-scatter.11.cloned.1.call-update) | async-done | bytes 262160 | tf_op jit(solution)/shard_map/reduce_scatter | solution.py:17
  110.9 1.0 convert_element_type.43
  111.9 0.8 copy.19
  112.7 5.7 %all-to-all-start.3 = ((bf16[64,2,512]{2,1,0:T(2,128)(2,1)}), bf16[64,2,512]{2,1,0:T(2,128)(2,1)}, u32[]{:S(2)}, u32[]{:S(2)}) async-start(bf16[64,2,512]{2,1,0:T(2,128)(2,1)} %copy.19), calls=%async_computation.7 | async-start | bytes 262144 | tf_op jit(solution)/shard_map/all_to_all | solution.py:20
  118.4 0.0 all-gather.3.cloned.1.call-start
  118.4 0.1 copy.27
  118.5 0.1 all_to_all.63
  118.6 6.4 %all_gather.20 = bf16[4,32,1024]{2,1,0:T(8,128)(2,1)S(1)} all-gather(bf16[4,32,512]{2,1,0:T(8,128)(2,1)S(1)} %all_to_all.63), channel_id=1, replica_groups=mesh['dp'=16,'tensor'=2] {'tensor'}, dimensions={2}, use_global_device_ids=true | all-gather | bytes 393216 | tf_op jit(solution)/shard_map/all_gather | solution.py:21
  125.0 0.4 multiply_reduce_fusion.1
  125.4 4.9 %psum.15 = f32[4,32]{1,0:T(4,128)S(1)} all-reduce(f32[4,32]{1,0:T(4,128)S(1)} %get-tuple-element.8), channel_id=1, replica_groups=mesh['dp'=16,'tensor'=2] {'tensor'}, use_global_device_ids=true, to_apply=%region_12.0 | all-reduce | flops 128 | bytes 1024 | tf_op jit(solution)/shard_map/psum | solution.py:65
  130.3 0.0 all-to-all-done.3
  130.3 1.7 copy.26
  132.0 1.0 all_to_all.67
  133.0 5.8 %all_gather.21 = bf16[4,32,1024]{2,1,0:T(8,128)(2,1)S(1)} all-gather(bf16[4,32,512]{2,1,0:T(8,128)(2,1)S(1)} %all_to_all.67), channel_id=1, replica_groups=mesh['dp'=16,'tensor'=2] {'tensor'}, dimensions={2}, use_global_device_ids=true | all-gather | bytes 393216 | tf_op jit(solution)/shard_map/all_gather | solution.py:21
  138.8 0.3 convolution_bitcast_fusion.6
  139.1 2.0 convolution_bitcast_fusion.4
  141.0 0.0 all-gather.3.cloned.1.call-update
  141.0 0.0 copy-start.5
  141.1 5.8 %convolution_convert_fusion.1 = bf16[2,1024,2048]{2,1,0:T(8,128)(2,1)} fusion(bf16[64,2,1024]{2,0,1:T(8,128)(2,1)S(1)} %all_gather.19, bf16[64,2,2048]{2,0,1:T(8,128)(2,1)S(1)} %fusion.16), kind=kOutput, calls=%fused_computation.3 | convolution fusion | flops 541065216 | bytes 9175040 | tf_op jit(solution)/shard_map/ied,ief->edf/dot_general | solution.py:58
  146.8 5.8 %convolution_convert_fusion = bf16[2,2048,1024]{2,1,0:T(8,128)(2,1)} fusion(bf16[64,2,1024]{2,0,1:T(8,128)(2,1)S(1)} %copy-done.4, f32[64,2,2048]{2,0,1:T(8,128)S(1)} %convolution_bitcast_fusion), kind=kOutput, calls=%fused_computation.2 | convolution fusion | flops 543424512 | bytes 9699328 | tf_op jit(solution)/shard_map/ief,ied->efd/dot_general | solution.py:55
  152.6 1.4 fusion.9
  154.0 1.3 fusion.2
  155.3 48.4 %all-gather.3.cloned.1.call-done = f32[32768,32]{0,1:T(8,128)} async-done(((f32[1024,32]{0,1:T(8,128)}), f32[32768,32]{0,1:T(8,128)}) %all-gather.3.cloned.1.call-update) | async-done | bytes 4194320 | tf_op jit(solution)/shard_map/all_gather | solution.py:78
  203.6 4.6 %copy.21 = f32[4,8,32,1024]{3,2,1,0:T(8,128)S(1)} copy(f32[4,8,32,1024]{3,1,2,0:T(8,128)} %bitcast.73) | data formatting | bytes 8388608
  208.3 1.3 bitcast_reduce_fusion
  (17 shorter events, 0.2 us)
Async XLA Ops:
  7.2 1.1 copy-start
  7.2 22.7 %reduce-scatter.5.cloned.1.call-start = ((), (), s32[]{:S(2)}) async-start(), calls=%async_computation.8 | async-start | bytes 786432 | tf_op jit(solution)/shard_map/reduce_scatter | solution.py:8
  12.3 35.0 %reduce-scatter.7.cloned.1.call-start = ((), (), s32[]{:S(2)}) async-start(), calls=%async_computation.9 | async-start | bytes 786432 | tf_op jit(solution)/shard_map/reduce_scatter | solution.py:8
  31.6 17.5 %all-to-all-start = ((bf16[4,32,512]{2,0,1:T(4,128)(2,1)}), bf16[4,32,512]{2,0,1:T(4,128)(2,1)S(1)}, u32[]{:S(2)}, u32[]{:S(2)}) async-start(bf16[4,32,512]{2,0,1:T(4,128)(2,1)} %copy.13), calls=%async_computation.1 | async-start | bytes 262144 | tf_op jit(solution)/shard_map/all_to_all | solution.py:11
  49.1 13.5 %all-to-all-start.1 = ((bf16[4,32,512]{2,0,1:T(4,128)(2,1)}), bf16[4,32,512]{2,0,1:T(4,128)(2,1)S(1)}, u32[]{:S(2)}, u32[]{:S(2)}) async-start(bf16[4,32,512]{2,0,1:T(4,128)(2,1)} %copy.15), calls=%async_computation.3 | async-start | bytes 262144 | tf_op jit(solution)/shard_map/all_to_all | solution.py:11
  54.7 38.9 %reduce-scatter.9.cloned.1.call-start = ((), (), s32[]{:S(2)}) async-start(), calls=%async_computation.10 | async-start | bytes 786432 | tf_op jit(solution)/shard_map/reduce_scatter | solution.py:17
  61.3 15.2 %copy-start.3 = (bf16[64,2,1024]{2,0,1:T(8,128)(2,1)}, bf16[64,2,1024]{2,0,1:T(8,128)(2,1)S(1)}, u32[]{:S(2)}) copy-start(bf16[64,2,1024]{2,0,1:T(8,128)(2,1)S(1)} %all_gather.18) | copy-start | bytes 786436
  62.7 10.9 %copy-start.1 = (bf16[2,2048,1024]{2,1,0:T(8,128)(2,1)S(1)}, bf16[2,2048,1024]{2,1,0:T(8,128)(2,1)}, u32[]{:S(2)}) copy-start(bf16[2,2048,1024]{2,1,0:T(8,128)(2,1)} %param.9) | copy-start | bytes 25165828
  62.7 13.8 %slice-start = ((s8[8388608]{0:T(1024)(128)(4,1)}), s8[4194304]{0:T(1024)(128)(4,1)S(1)}, s32[]{:S(2)}) async-start(s8[8388608]{0:T(1024)(128)(4,1)} %bitcast.71), calls=%async_computation.13 | async-start | bytes 8388608
  68.5 8.0 %slice-start.1 = ((s8[8388608]{0:T(1024)(128)(4,1)}), s8[4194304]{0:T(1024)(128)(4,1)S(1)}, s32[]{:S(2)}) async-start(s8[8388608]{0:T(1024)(128)(4,1)} %bitcast.71), calls=%async_computation.14 | async-start | bytes 8388608
  80.0 58.8 %copy-start.2 = (bf16[4,72,1024]{2,1,0:T(8,128)(2,1)S(1)}, bf16[4,72,1024]{2,1,0:T(8,128)(2,1)}, u32[]{:S(2)}) copy-start(bf16[4,72,1024]{2,1,0:T(8,128)(2,1)} %param.6) | copy-start | bytes 1769476
  80.0 30.9 %reduce-scatter.11.cloned.1.call-start = ((), (), s32[]{:S(2)}) async-start(), calls=%async_computation.11 | async-start | bytes 786432 | tf_op jit(solution)/shard_map/reduce_scatter | solution.py:17
  95.3 17.4 %all-to-all-start.2 = ((bf16[64,2,512]{2,1,0:T(2,128)(2,1)}), bf16[64,2,512]{2,1,0:T(2,128)(2,1)S(1)}, u32[]{:S(2)}, u32[]{:S(2)}) async-start(bf16[64,2,512]{2,1,0:T(2,128)(2,1)} %copy.17), calls=%async_computation.5 | async-start | bytes 262144 | tf_op jit(solution)/shard_map/all_to_all | solution.py:20
  112.7 17.6 %all-to-all-start.3 = ((bf16[64,2,512]{2,1,0:T(2,128)(2,1)}), bf16[64,2,512]{2,1,0:T(2,128)(2,1)}, u32[]{:S(2)}, u32[]{:S(2)}) async-start(bf16[64,2,512]{2,1,0:T(2,128)(2,1)} %copy.19), calls=%async_computation.7 | async-start | bytes 262144 | tf_op jit(solution)/shard_map/all_to_all | solution.py:20
  118.4 85.2 %all-gather.3.cloned.1.call-start = ((), (), s32[]{:S(2)}) async-start(), calls=%async_computation.12 | async-start | bytes 4325376 | tf_op jit(solution)/shard_map/all_gather | solution.py:78
  139.1 7.8 %copy-start.4 = (bf16[64,2,1024]{2,0,1:T(8,128)(2,1)S(1)}, bf16[64,2,1024]{2,0,1:T(8,128)(2,1)}, u32[]{:S(2)}) copy-start(bf16[64,2,1024]{2,0,1:T(8,128)(2,1)} %copy-done.3) | copy-start | bytes 786436
  141.0 11.6 %copy-start.5 = (bf16[1024,32]{0,1:T(8,128)(2,1)S(1)}, bf16[1024,32]{0,1:T(8,128)(2,1)}, u32[]{:S(2)}) copy-start(bf16[1024,32]{0,1:T(8,128)(2,1)} %param.7) | copy-start | bytes 196612
Sparse Core Ops, SparseCore 0:
  12.4 17.3 reduce-scatter.4
  32.7 14.6 reduce-scatter.6
  80.1 13.4 reduce-scatter.8
  96.3 14.6 reduce-scatter.10
  141.2 62.4 all-gather.2
